TPU v7x, 32 devices: a whole 2x2x4 slice. The times are simulated.
32 devices in a mesh: zero: 8 (over y, x, core), width: 4 (over z).
Axes of the slice: x: 2, y: 2, z: 4, core: 2. Of those that a mesh axis runs over, the one named last changes fastest.
Arguments:
- w_gate: bfloat16 [3072, 8192], P('zero', 'width'), may hold values from -0.109375 to 0.109375
- low_gate: bfloat16 [3072, 16], P('zero'), may hold values from -0.109375 to 0.109375
- high_gate: bfloat16 [16, 8192], P(None, 'width'), may hold values from -1.5 to 1.5
- w_up: bfloat16 [3072, 8192], P('zero', 'width'), may hold values from -0.109375 to 0.109375
- low_up: bfloat16 [3072, 16], P('zero'), may hold values from -0.109375 to 0.109375
- high_up: bfloat16 [16, 8192], P(None, 'width'), may hold values from -1.5 to 1.5
- norm_train: float32 [3072], P(('zero', 'width')), may hold values from 0.25 to 1.75
- norm_step: float32 [3072], P(('zero', 'width')), may hold values from -0.3 to 0.3
Outputs:
- serving_gate: bfloat16 [8192, 3072], P('width')
- serving_up: bfloat16 [8192, 3072], P('width')
- serve_norm: bfloat16 [3072], replicated
All inputs are finite; a program needn't handle non-finite values.
Results may differ from a plain program's by a relative error of at most 0.001.
Values may be sent and summed in bfloat16 or wider, within the bound.
A program may use at most 128 MiB of HBM per device.

v0:
```python
import jax
import jax.numpy as jnp
from jax import lax
from jax.sharding import PartitionSpec as P

mix_rate = 1.0


def on_device(w_gate, low_gate, high_gate, w_up, low_up, high_up, norm_train, norm_step):
    whole_gate = w_gate.astype(jnp.float32) + mix_rate * jnp.dot(
        low_gate, high_gate, preferred_element_type=jnp.float32
    )
    whole_up = w_up.astype(jnp.float32) + mix_rate * jnp.dot(
        low_up, high_up, preferred_element_type=jnp.float32
    )
    narrow_gate, narrow_up = (whole_gate.astype(jnp.bfloat16), whole_up.astype(jnp.bfloat16))
    serving_gate, serving_up = (
        lax.all_gather(narrow_gate, "zero", axis=0, tiled=True),
        lax.all_gather(narrow_up, "zero", axis=0, tiled=True),
    )
    serving_gate, serving_up = (serving_gate.T, serving_up.T)
    serve_norm = lax.all_gather(
        (norm_train + norm_step).astype(jnp.bfloat16), ("zero", "width"), axis=0, tiled=True
    )
    return (serving_gate, serving_up, serve_norm)


def solution(mesh):
    placed = (
        P("zero", "width"),
        P("zero", None),
        P(None, "width"),
        P("zero", "width"),
        P("zero", None),
        P(None, "width"),
        P(("zero", "width")),
        P(("zero", "width")),
    )
    return jax.shard_map(
        on_device,
        mesh=mesh,
        in_specs=placed,
        out_specs=(P("width", None), P("width", None), P()),
        check_vma=False,
    )
```

profile of v0, /device:TPU:0, one launch (start us, length us, event | category | flops | bytes accessed | tf_op | source)
XLA Modules:
  0.0 184.2 jit_solution(14014861292981625243)
XLA Ops:
  7.2 0.0 copy-start
  7.2 0.0 copy-start.1
  7.2 0.0 copy-start.3
  7.2 0.0 copy-start.2
  7.2 0.0 all-gather.3.cloned.1.call-start
  7.3 0.8 copy-done
  8.0 3.2 %add_convert_fusion.1 = bf16[384,2048]{1,0:T(8,128)(2,1)} fusion(bf16[384,2048]{1,0:T(8,128)(2,1)} %param.8, bf16[384,16]{0,1:T(8,128)(2,1)} %param.9, bf16[16,2048]{1,0:T(8,128)(2,1)S(1)} %copy-done), kind=kOutput, calls=%fused_computation.1 | convolution fusion | flops 27525120 | bytes 3223552 | tf_op jit(solution)/shard_map/dot_general | solution.py:10
  11.2 0.0 copy-start.4
  11.2 0.0 copy-start.5
  11.2 0.0 all-gather.3.cloned.1.call-update
  11.2 0.0 all-gather.5.cloned.1.call-start
  11.2 0.0 copy-done.1
  11.3 0.0 copy-done.3
  11.3 0.0 copy-done.2
  11.3 1.8 add_convert_fusion
  13.1 0.0 all-gather.5.cloned.1.call-update
  13.1 0.0 copy-done.4
  13.1 0.0 copy-done.5
  13.1 0.2 dynamic-update-slice
  13.4 42.7 %all-reduce = bf16[3072]{0:T(1024)(128)(2,1)} all-reduce(bf16[3072]{0:T(1024)(128)(2,1)S(1)} %dynamic-update-slice), channel_id=1, replica_groups=mesh['zero'=8,'width'=4] {'zero','width'}, use_global_device_ids=true, to_apply=%add | all-reduce | flops 3072 | bytes 12288
  56.1 30.8 %all-gather.3.cloned.1.call-done = bf16[3072,2048]{1,0:T(8,128)(2,1)} async-done(((bf16[384,2048]{1,0:T(8,128)(2,1)}), bf16[3072,2048]{1,0:T(8,128)(2,1)}) %all-gather.3.cloned.1.call-update) | async-done | bytes 12582928 | tf_op jit(solution)/shard_map/all_gather | solution.py:18
  86.9 16.8 %copy.11 = bf16[2048,3072]{1,0:T(8,128)(2,1)} copy(bf16[2048,3072]{0,1:T(8,128)(2,1)} %bitcast.6) | data formatting | bytes 25165824
  103.7 57.1 %all-gather.5.cloned.1.call-done = bf16[3072,2048]{1,0:T(8,128)(2,1)} async-done(((bf16[384,2048]{1,0:T(8,128)(2,1)}), bf16[3072,2048]{1,0:T(8,128)(2,1)}) %all-gather.5.cloned.1.call-update) | async-done | bytes 12582928 | tf_op jit(solution)/shard_map/all_gather | solution.py:19
  160.8 16.6 %copy.12 = bf16[2048,3072]{1,0:T(8,128)(2,1)} copy(bf16[2048,3072]{0,1:T(8,128)(2,1)} %bitcast.7) | data formatting | bytes 25165824
  (2 shorter events, 0.0 us)
Async XLA Ops:
  7.2 0.8 copy-start
  7.2 4.1 %copy-start.1 = (bf16[384,2048]{1,0:T(8,128)(2,1)S(1)}, bf16[384,2048]{1,0:T(8,128)(2,1)}, u32[]{:S(2)}) copy-start(bf16[384,2048]{1,0:T(8,128)(2,1)} %param.11) | copy-start | bytes 4718596
  7.2 4.1 %copy-start.3 = (bf16[384,16]{0,1:T(8,128)(2,1)S(1)}, bf16[384,16]{0,1:T(8,128)(2,1)}, u32[]{:S(2)}) copy-start(bf16[384,16]{0,1:T(8,128)(2,1)} %param.12) | copy-start | bytes 36868
  7.2 4.1 %copy-start.2 = (bf16[16,2048]{1,0:T(8,128)(2,1)S(1)}, bf16[16,2048]{1,0:T(8,128)(2,1)}, u32[]{:S(2)}) copy-start(bf16[16,2048]{1,0:T(8,128)(2,1)} %param.13) | copy-start | bytes 196612
  7.2 79.7 %all-gather.3.cloned.1.call-start = ((), (), s32[]{:S(2)}) async-start(), calls=%async_computation | async-start | bytes 14155776 | tf_op jit(solution)/shard_map/all_gather | solution.py:18
  11.2 1.9 %copy-start.4 = (f32[96]{0:T(128)S(1)}, f32[96]{0:T(128)}, u32[]{:S(2)}) copy-start(f32[96]{0:T(128)} %param.14) | copy-start | bytes 1156
  11.2 1.9 %copy-start.5 = (f32[96]{0:T(128)S(1)}, f32[96]{0:T(128)}, u32[]{:S(2)}) copy-start(f32[96]{0:T(128)} %param.15) | copy-start | bytes 1156
  11.2 149.6 %all-gather.5.cloned.1.call-start = ((), (), s32[]{:S(2)}) async-start(), calls=%async_computation.1 | async-start | bytes 14155776 | tf_op jit(solution)/shard_map/all_gather | solution.py:19
Sparse Core Ops, SparseCore 0:
  11.3 75.5 all-gather.2
  88.8 71.8 all-gather.4
where the time goes:
time: 185 us; the launch traced here: 184 us
  waiting for transfers between devices  87.9 us (48%)
  blocking collectives  42.7 us (23%)
  local copies, waits for them, and re-layouts  34.4 us (19%)
  between operations  14.1 us (8%)
  matrix products  4.95 us (3%)
    all_gather x1, waiting for transfers between devices, on_device(): lax.all_gather(narrow_up, 'zero', axis=0, tiled=True)  57.1 us
    unnamed x1, blocking collectives  42.7 us
    unnamed x16, local copies, waits for them, and re-layouts  34.4 us
    all_gather x1, waiting for transfers between devices, on_device(): lax.all_gather(narrow_gate, 'zero', axis=0, tiled=True)  30.8 us
  transfers between devices with their start and end apart: 2, of which 2 were waited for; matrix products, arithmetic and copies ran while one was open for 10% of the time, Pallas kernels for 0%

commit v1 on v0

v1 whole, which is shorter than its diff:
```python
import functools

import jax
import jax.numpy as jnp
from jax import lax
from jax.experimental import pallas as pl
from jax.experimental.pallas import tpu as pltpu
from jax.sharding import PartitionSpec as P

mix_rate = 1.0
MESH = pl.DeviceIdType.MESH
CHUNK = 256


def merge_kernel(
    n_zero, n_width, w_gate, low_gate, high_gate, w_up, low_up, high_up, step_a, step_b,
    held, gains, w, low, high, gain, load_sem, gain_send, gain_recv, send_sem, recv_sem,
):
    zero, width = lax.axis_index("zero"), lax.axis_index("width")
    core = lax.rem(zero, 2)
    partner = zero + 1 - 2 * core
    chip = zero // 2
    cx, cy = lax.rem(chip, 2), chip // 2
    over_x = zero + 2 * (1 - 2 * cx)
    over_y = zero + 4 * (1 - 2 * cy)
    first = over_x + core * (over_y - over_x)
    second = over_y + core * (over_x - over_y)
    across = over_x + over_y - zero
    their_first = second + partner - zero
    their_second = first + partner - zero
    their_across = across + partner - zero

    loads = [
        pltpu.make_async_copy(src, dst, load_sem.at[i])
        for i, (src, dst) in enumerate(
            [
                (w_gate, w.at[0]), (low_gate, low.at[0]), (high_gate, high.at[0]),
                (w_up, w.at[1]), (low_up, low.at[1]), (high_up, high.at[1]),
            ]
        )
    ]
    for load in loads:
        load.start()
    gain[...] = step_a[...] + step_b[...]

    n = n_zero * n_width
    flat = zero * n_width + width

    def other(d):
        t = lax.rem(flat + d, n)
        return {"zero": t // n_width, "width": lax.rem(t, n_width)}

    barrier = pltpu.get_barrier_semaphore()

    def greet(d, _):
        pl.semaphore_signal(barrier, inc=1, device_id=other(d), device_id_type=MESH)
        return _

    lax.fori_loop(1, n, greet, 0)
    gains[flat] = gain[...]
    for load in loads:
        load.wait()

    rows = held.shape[2]
    per = rows // CHUNK
    count = 2 * per

    def at(block, i):
        return held.at[block, i // per, pl.ds(pl.multiple_of(lax.rem(i, per) * CHUNK, CHUNK), CHUNK)]

    def make(i):
        a = i // per
        cols = pl.ds(pl.multiple_of(lax.rem(i, per) * CHUNK, CHUNK), CHUNK)
        delta = lax.dot_general(
            high[a, :, cols], low[a], (((0,), (0,)), ((), ())),
            preferred_element_type=jnp.float32,
        )
        base = w[a, :, cols].T.astype(jnp.float32)
        held[zero, a, cols] = (base + mix_rate * delta).astype(held.dtype)

    def copy(flow, block, i, target):
        return pltpu.make_async_remote_copy(
            src_ref=at(block, i), dst_ref=at(block, i),
            send_sem=send_sem.at[flow, i], recv_sem=recv_sem.at[flow, i],
            device_id={"zero": target}, device_id_type=MESH,
        )

    def send_own(i):
        copy(1, zero, i, first).start()
        copy(2, zero, i, second).start()
        copy(0, zero, i, partner).start()

    make(0)
    pl.semaphore_wait(barrier, n - 1)

    def make_and_send(i, _):
        make(i)
        send_own(i - 1)
        return _

    lax.fori_loop(1, count, make_and_send, 0)
    send_own(count - 1)

    def gain_copy(d, slot):
        return pltpu.make_async_remote_copy(
            src_ref=gain, dst_ref=gains.at[slot],
            send_sem=gain_send.at[d], recv_sem=gain_recv.at[d],
            device_id=other(d), device_id_type=MESH,
        )

    def send_gain(d, _):
        gain_copy(d, flat).start()
        return _

    lax.fori_loop(1, n, send_gain, 0)

    def relay(i, _):
        copy(1, first, i, first).wait_recv()
        copy(3, first, i, second).start()
        copy(4, first, i, partner).start()
        copy(2, second, i, second).wait_recv()
        copy(5, second, i, partner).start()
        return _

    lax.fori_loop(0, count, relay, 0)

    def pass_on(i, _):
        copy(3, across, i, second).wait_recv()
        copy(6, across, i, partner).start()
        return _

    lax.fori_loop(0, count, pass_on, 0)

    def end_gain(d, _):
        gain_copy(d, lax.rem(flat + n - d, n)).wait()
        return _

    lax.fori_loop(1, n, end_gain, 0)

    def end(i, _):
        copy(0, partner, i, partner).wait_recv()
        copy(4, their_first, i, partner).wait_recv()
        copy(5, their_second, i, partner).wait_recv()
        copy(6, their_across, i, partner).wait_recv()
        copy(0, zero, i, partner).wait_send()
        copy(1, zero, i, first).wait_send()
        copy(2, zero, i, second).wait_send()
        copy(3, first, i, second).wait_send()
        copy(4, first, i, partner).wait_send()
        copy(5, second, i, partner).wait_send()
        copy(6, across, i, partner).wait_send()
        return _

    lax.fori_loop(0, count, end, 0)


def flush_kernel(held, out_gate, out_up, sem):
    blocks, _, _, depth = held.shape
    copies = [
        pltpu.make_async_copy(
            held.at[b, a], out.at[:, pl.ds(b * depth, depth)], sem.at[b, a]
        )
        for a, out in enumerate((out_gate, out_up))
        for b in range(blocks)
    ]
    for c in copies:
        c.start()
    for c in copies:
        c.wait()


def by_kernels(n_zero, n_width, w_gate, low_gate, high_gate, w_up, low_up, high_up, norm_train, norm_step):
    depth, rows = w_gate.shape
    rank = high_gate.shape[0]
    share = norm_train.shape[0]
    n = n_zero * n_width
    count = 2 * (rows // CHUNK)
    anywhere = pl.BlockSpec(memory_space=pl.ANY)
    vmem = pl.BlockSpec(memory_space=pltpu.VMEM)
    dma = pltpu.SemaphoreType.DMA
    held, gains = pl.pallas_call(
        functools.partial(merge_kernel, n_zero, n_width),
        out_shape=(
            pltpu.VMEM((n_zero, 2, rows, depth), jnp.bfloat16),
            pltpu.VMEM((n, 1, share), jnp.float32),
        ),
        in_specs=[anywhere] * 6 + [vmem] * 2,
        out_specs=(vmem, vmem),
        scratch_shapes=[
            pltpu.VMEM((2, depth, rows), jnp.bfloat16),
            pltpu.VMEM((2, rank, depth), jnp.bfloat16),
            pltpu.VMEM((2, rank, rows), jnp.bfloat16),
            pltpu.VMEM((1, share), jnp.float32),
            dma((6,)),
            dma((n,)),
            dma((n,)),
            dma((7, count)),
            dma((7, count)),
        ],
        compiler_params=pltpu.CompilerParams(
            collective_id=0, has_side_effects=True, vmem_limit_bytes=34 * 2**20
        ),
    )(
        w_gate, low_gate.T, high_gate, w_up, low_up.T, high_up,
        norm_train.reshape(1, share), norm_step.reshape(1, share),
    )
    out = jax.ShapeDtypeStruct((rows, n_zero * depth), jnp.bfloat16)
    serving_gate, serving_up = pl.pallas_call(
        flush_kernel,
        out_shape=(out, out),
        in_specs=[vmem],
        out_specs=(anywhere, anywhere),
        scratch_shapes=[dma((n_zero, 2))],
        compiler_params=pltpu.CompilerParams(vmem_limit_bytes=34 * 2**20),
    )(pltpu.with_memory_space_constraint(held, pltpu.VMEM))
    return serving_gate, serving_up, gains.reshape(n * share).astype(jnp.bfloat16)


def by_gathers(w_gate, low_gate, high_gate, w_up, low_up, high_up, norm_train, norm_step):
    def merged(w, low, high):
        whole = w.astype(jnp.float32) + mix_rate * jnp.dot(
            low, high, preferred_element_type=jnp.float32
        )
        return lax.all_gather(whole.astype(jnp.bfloat16), "zero", axis=0, tiled=True).T

    serve_norm = lax.all_gather(
        (norm_train + norm_step).astype(jnp.bfloat16), ("zero", "width"), axis=0, tiled=True
    )
    return merged(w_gate, low_gate, high_gate), merged(w_up, low_up, high_up), serve_norm


def solution(mesh):
    n_zero, n_width = mesh.shape["zero"], mesh.shape["width"]
    planar = n_zero == 2 * 2 * 2
    body = functools.partial(by_kernels, n_zero, n_width) if planar else by_gathers
    placed = (
        P("zero", "width"),
        P("zero", None),
        P(None, "width"),
        P("zero", "width"),
        P("zero", None),
        P(None, "width"),
        P(("zero", "width")),
        P(("zero", "width")),
    )
    return jax.shard_map(
        body,
        mesh=mesh,
        in_specs=placed,
        out_specs=(P("width", None), P("width", None), P()),
        check_vma=False,
    )
```

time: 185 us -> 125 us (0.68)
  Pallas kernels: 0 us -> 123 us
  waiting for transfers between devices: 87.9 us -> 0 us
  blocking collectives: 42.7 us -> 0 us
  local copies, waits for them, and re-layouts: 34.4 us -> 0.68 us
  between operations: 14.1 us -> 0.65 us
  matrix products: 4.95 us -> 0 us
    pallas_call x0 -> x2, Pallas kernels: none -> 123 us  [the longest x1 115 us: by_kernels(): pl.pallas_call(functools.partial(merge_kernel, n_zero, n_width), out_shap...]
    all_gather x2 -> x0, waiting for transfers between devices: 87.9 us -> none  [the longest x1 57.1 us: on_device(): lax.all_gather(narrow_up, 'zero', axis=0, tiled=True)]
    unnamed x1 -> x0, blocking collectives: 42.7 us -> none
    unnamed x16 -> x0, local copies, waits for them, and re-layouts: 34.4 us -> none
    dot_general x2 -> x0, matrix products: 4.95 us -> none  [the longest x1 3.16 us: on_device(): jnp.dot(low_gate, high_gate, preferred_element_type=jnp.float32)]
  transfers between devices with their start and end apart: 2 -> 0, of which waited for: 2 -> 0; matrix products, arithmetic and copies ran while one was open for 10% -> 0% of each run, Pallas kernels for 0% -> 0%
where the time goes in v1:
time: 125 us
  Pallas kernels  123 us (98%)
    pallas_call x1, Pallas kernels, by_kernels(): pl.pallas_call(functools.partial(merge_kernel, n_zero, n_width), out_shap...  115 us
    pallas_call x1, Pallas kernels, by_kernels(): pl.pallas_call(flush_kernel, out_shape=(out, out), in_specs=[vmem], out_s...  8.51 us

profile of v1, /device:TPU:0, one launch (start us, length us, event | category | flops | bytes accessed | tf_op | source)
XLA Modules:
  0.0 124.7 jit_solution(15031468589948919489)
XLA Ops:
  0.6 114.8 %shard_map.103 = (bf16[8,2,2048,384]{3,2,1,0:T(8,128)(2,1)S(1)}, f32[32,1,96]{2,1,0:T(1,128)S(1)}) custom-call(bf16[384,2048]{1,0:T(8,128)(2,1)} %w_gate.1, bf16[16,384]{1,0:T(8,128)(2,1)} %bitcast.4, bf16[16,2048]{1,0:T(8,128)(2,1)} %high_gate.1, bf16[384,2048]{1,0:T(8,128)(2,1)} %w_up.1, bf16[16,384]{1,0:T(8,128)(2,1)} %bitcast.5, ...), custom_call_target="tpu_custom_call" | custom-call | tf_op jit(solution)/shard_map/pallas_call | solution.py:181
  115.4 8.5 %shard_map.104 = (bf16[2048,3072]{1,0:T(8,128)(2,1)}, bf16[2048,3072]{1,0:T(8,128)(2,1)}) custom-call(bf16[8,2,2048,384]{3,2,1,0:T(8,128)(2,1)S(1)} %get-tuple-element.7.held), custom_call_target="tpu_custom_call" | custom-call | tf_op jit(solution)/shard_map/pallas_call | solution.py:208
  124.0 0.1 convert_reduce_fusion
  124.0 0.7 convert_element_type.7

commit v2 on v1

--- a/solution.py
+++ b/solution.py
@@ -9,12 +9,12 @@
 
 mix_rate = 1.0
 MESH = pl.DeviceIdType.MESH
-CHUNK = 256
+PIECES = 4
 
 
 def merge_kernel(
     n_zero, n_width, w_gate, low_gate, high_gate, w_up, low_up, high_up, step_a, step_b,
-    held, gains, w, low, high, gain, load_sem, gain_send, gain_recv, send_sem, recv_sem,
+    held, gains, w, low, high, load_sem, gain_send, gain_recv, send_sem, recv_sem,
 ):
     zero, width = lax.axis_index("zero"), lax.axis_index("width")
     core = lax.rem(zero, 2)
@@ -30,6 +30,18 @@
     their_second = first + partner - zero
     their_across = across + partner - zero
 
+    flat = zero * n_width + width
+    spans = [1 << b for b in range(n_width.bit_length() - 1)]
+
+    def beside(span):
+        return width + span * (1 - 2 * lax.rem(width // span, 2))
+
+    barrier = pltpu.get_barrier_semaphore()
+    for target in (partner, first, second):
+        pl.semaphore_signal(barrier, inc=1, device_id={"zero": target}, device_id_type=MESH)
+    for span in spans:
+        pl.semaphore_signal(barrier, inc=1, device_id={"width": beside(span)}, device_id_type=MESH)
+
     loads = [
         pltpu.make_async_copy(src, dst, load_sem.at[i])
         for i, (src, dst) in enumerate(
@@ -41,36 +53,21 @@
     ]
     for load in loads:
         load.start()
-    gain[...] = step_a[...] + step_b[...]
-
-    n = n_zero * n_width
-    flat = zero * n_width + width
-
-    def other(d):
-        t = lax.rem(flat + d, n)
-        return {"zero": t // n_width, "width": lax.rem(t, n_width)}
-
-    barrier = pltpu.get_barrier_semaphore()
-
-    def greet(d, _):
-        pl.semaphore_signal(barrier, inc=1, device_id=other(d), device_id_type=MESH)
-        return _
-
-    lax.fori_loop(1, n, greet, 0)
-    gains[flat] = gain[...]
-    for load in loads:
+    gains[flat] = step_a[...] + step_b[...]
+    for load in loads[:3]:
         load.wait()
 
     rows = held.shape[2]
-    per = rows // CHUNK
+    per = PIECES
+    chunk = rows // per
     count = 2 * per
 
     def at(block, i):
-        return held.at[block, i // per, pl.ds(pl.multiple_of(lax.rem(i, per) * CHUNK, CHUNK), CHUNK)]
+        return held.at[block, i // per, pl.ds(pl.multiple_of(lax.rem(i, per) * chunk, chunk), chunk)]
 
     def make(i):
         a = i // per
-        cols = pl.ds(pl.multiple_of(lax.rem(i, per) * CHUNK, CHUNK), CHUNK)
+        cols = pl.ds(pl.multiple_of(lax.rem(i, per) * chunk, chunk), chunk)
         delta = lax.dot_general(
             high[a, :, cols], low[a], (((0,), (0,)), ((), ())),
             preferred_element_type=jnp.float32,
@@ -91,28 +88,43 @@
         copy(0, zero, i, partner).start()
 
     make(0)
-    pl.semaphore_wait(barrier, n - 1)
+    make(1)
+    pl.semaphore_wait(barrier, 3 + len(spans))
+    send_own(0)
+    for load in loads[3:]:
+        load.wait()
 
     def make_and_send(i, _):
         make(i)
         send_own(i - 1)
         return _
 
-    lax.fori_loop(1, count, make_and_send, 0)
+    lax.fori_loop(2, count, make_and_send, 0)
     send_own(count - 1)
 
-    def gain_copy(d, slot):
+    def gain_beside(b, start):
+        span = spans[b]
+        own = gains.at[pl.ds(start // span * span, span)]
         return pltpu.make_async_remote_copy(
-            src_ref=gain, dst_ref=gains.at[slot],
-            send_sem=gain_send.at[d], recv_sem=gain_recv.at[d],
-            device_id=other(d), device_id_type=MESH,
-        )
-
-    def send_gain(d, _):
-        gain_copy(d, flat).start()
-        return _
-
-    lax.fori_loop(1, n, send_gain, 0)
+            src_ref=own, dst_ref=own, send_sem=gain_send.at[b], recv_sem=gain_recv.at[b],
+            device_id={"width": beside(span)}, device_id_type=MESH,
+        )
+
+    for b, span in enumerate(spans):
+        gain_beside(b, flat).start()
+        gain_beside(b, zero * n_width + beside(span)).wait_recv()
+
+    def gain_copy(flow, block, target):
+        part = gains.at[pl.ds(block * n_width, n_width)]
+        return pltpu.make_async_remote_copy(
+            src_ref=part, dst_ref=part,
+            send_sem=send_sem.at[flow, count], recv_sem=recv_sem.at[flow, count],
+            device_id={"zero": target}, device_id_type=MESH,
+        )
+
+    gain_copy(1, zero, first).start()
+    gain_copy(2, zero, second).start()
+    gain_copy(0, zero, partner).start()
 
     def relay(i, _):
         copy(1, first, i, first).wait_recv()
@@ -123,6 +135,11 @@
         return _
 
     lax.fori_loop(0, count, relay, 0)
+    gain_copy(1, first, first).wait_recv()
+    gain_copy(3, first, second).start()
+    gain_copy(4, first, partner).start()
+    gain_copy(2, second, second).wait_recv()
+    gain_copy(5, second, partner).start()
 
     def pass_on(i, _):
         copy(3, across, i, second).wait_recv()
@@ -130,12 +147,15 @@
         return _
 
     lax.fori_loop(0, count, pass_on, 0)
-
-    def end_gain(d, _):
-        gain_copy(d, lax.rem(flat + n - d, n)).wait()
-        return _
-
-    lax.fori_loop(1, n, end_gain, 0)
+    gain_copy(3, across, second).wait_recv()
+    gain_copy(6, across, partner).start()
+
+    for flow, block in ((0, partner), (4, their_first), (5, their_second), (6, their_across)):
+        gain_copy(flow, block, partner).wait_recv()
+    for flow, block in enumerate((zero, zero, zero, first, first, second, across)):
+        gain_copy(flow, block, partner).wait_send()
+    for b in range(len(spans)):
+        gain_beside(b, flat).wait_send()
 
     def end(i, _):
         copy(0, partner, i, partner).wait_recv()
@@ -174,7 +194,7 @@
     rank = high_gate.shape[0]
     share = norm_train.shape[0]
     n = n_zero * n_width
-    count = 2 * (rows // CHUNK)
+    count = 2 * PIECES
     anywhere = pl.BlockSpec(memory_space=pl.ANY)
     vmem = pl.BlockSpec(memory_space=pltpu.VMEM)
     dma = pltpu.SemaphoreType.DMA
@@ -190,12 +210,11 @@
             pltpu.VMEM((2, depth, rows), jnp.bfloat16),
             pltpu.VMEM((2, rank, depth), jnp.bfloat16),
             pltpu.VMEM((2, rank, rows), jnp.bfloat16),
-            pltpu.VMEM((1, share), jnp.float32),
             dma((6,)),
-            dma((n,)),
-            dma((n,)),
-            dma((7, count)),
-            dma((7, count)),
+            dma((n_width.bit_length(),)),
+            dma((n_width.bit_length(),)),
+            dma((7, count + 1)),
+            dma((7, count + 1)),
         ],
         compiler_params=pltpu.CompilerParams(
             collective_id=0, has_side_effects=True, vmem_limit_bytes=34 * 2**20
@@ -231,7 +250,7 @@
 
 def solution(mesh):
     n_zero, n_width = mesh.shape["zero"], mesh.shape["width"]
-    planar = n_zero == 2 * 2 * 2
+    planar = n_zero == 2 * 2 * 2 and n_width & (n_width - 1) == 0
     body = functools.partial(by_kernels, n_zero, n_width) if planar else by_gathers
     placed = (
         P("zero", "width"),

time: 125 us -> 121 us (0.968)
  Pallas kernels: 123 us -> 119 us
    pallas_call x1, Pallas kernels: 115 us -> 111 us  [by_kernels(): pl.pallas_call(functools.partial(merge_kernel, n_zero, n_width), out_shap...]
where the time goes in v2:
time: 121 us; the launch traced here: 120 us
  Pallas kernels  119 us (98%)
    pallas_call x1, Pallas kernels, by_kernels(): pl.pallas_call(functools.partial(merge_kernel, n_zero, n_width), out_shap...  111 us
    pallas_call x1, Pallas kernels, by_kernels(): pl.pallas_call(flush_kernel, out_shape=(out, out), in_specs=[vmem], out_s...  8.51 us

profile of v2, /device:TPU:0, one launch (start us, length us, event | category | flops | bytes accessed | tf_op | source)
XLA Modules:
  0.0 120.5 jit_solution(1590100154401973805)
XLA Ops:
  0.6 110.6 %shard_map.103 = (bf16[8,2,2048,384]{3,2,1,0:T(8,128)(2,1)S(1)}, f32[32,1,96]{2,1,0:T(1,128)S(1)}) custom-call(bf16[384,2048]{1,0:T(8,128)(2,1)} %w_gate.1, bf16[16,384]{1,0:T(8,128)(2,1)} %bitcast.4, bf16[16,2048]{1,0:T(8,128)(2,1)} %high_gate.1, bf16[384,2048]{1,0:T(8,128)(2,1)} %w_up.1, bf16[16,384]{1,0:T(8,128)(2,1)} %bitcast.5, ...), custom_call_target="tpu_custom_call" | custom-call | tf_op jit(solution)/shard_map/pallas_call | solution.py:201
  111.2 8.5 %shard_map.104 = (bf16[2048,3072]{1,0:T(8,128)(2,1)}, bf16[2048,3072]{1,0:T(8,128)(2,1)}) custom-call(bf16[8,2,2048,384]{3,2,1,0:T(8,128)(2,1)S(1)} %get-tuple-element.7.held), custom_call_target="tpu_custom_call" | custom-call | tf_op jit(solution)/shard_map/pallas_call | solution.py:227
  119.7 0.1 convert_reduce_fusion
  119.8 0.7 convert_element_type.7

commit v3 on v2

--- a/solution.py
+++ b/solution.py
@@ -42,12 +42,15 @@
     for span in spans:
         pl.semaphore_signal(barrier, inc=1, device_id={"width": beside(span)}, device_id_type=MESH)
 
+    piece = w.shape[2] // PIECES
+    parts = [pl.ds(i * piece, piece) for i in range(PIECES)]
     loads = [
         pltpu.make_async_copy(src, dst, load_sem.at[i])
         for i, (src, dst) in enumerate(
             [
-                (w_gate, w.at[0]), (low_gate, low.at[0]), (high_gate, high.at[0]),
-                (w_up, w.at[1]), (low_up, low.at[1]), (high_up, high.at[1]),
+                (low_gate, low.at[0]), (high_gate, high.at[0]),
+                *[(w_gate.at[:, part], w.at[0, :, part]) for part in parts],
+                (low_up, low.at[1]), (high_up, high.at[1]), (w_up, w.at[1]),
             ]
         )
     ]
@@ -88,10 +91,11 @@
         copy(0, zero, i, partner).start()
 
     make(0)
+    loads[3].wait()
     make(1)
     pl.semaphore_wait(barrier, 3 + len(spans))
     send_own(0)
-    for load in loads[3:]:
+    for load in loads[4:]:
         load.wait()
 
     def make_and_send(i, _):
@@ -210,7 +214,7 @@
             pltpu.VMEM((2, depth, rows), jnp.bfloat16),
             pltpu.VMEM((2, rank, depth), jnp.bfloat16),
             pltpu.VMEM((2, rank, rows), jnp.bfloat16),
-            dma((6,)),
+            dma((5 + PIECES,)),
             dma((n_width.bit_length(),)),
             dma((n_width.bit_length(),)),
             dma((7, count + 1)),

time: 121 us -> 121 us (level)
  no operation moved by 1% of the time
where the time goes in v3:
time: 121 us; the launch traced here: 120 us
  Pallas kernels  119 us (98%)
    pallas_call x1, Pallas kernels, by_kernels(): pl.pallas_call(functools.partial(merge_kernel, n_zero, n_width), out_shap...  111 us
    pallas_call x1, Pallas kernels, by_kernels(): pl.pallas_call(flush_kernel, out_shape=(out, out), in_specs=[vmem], out_s...  8.51 us

profile of v3, /device:TPU:0, one launch (start us, length us, event | category | flops | bytes accessed | tf_op | source)
XLA Modules:
  0.0 120.5 jit_solution(6625793271095616481)
XLA Ops:
  0.6 110.6 %shard_map.103 = (bf16[8,2,2048,384]{3,2,1,0:T(8,128)(2,1)S(1)}, f32[32,1,96]{2,1,0:T(1,128)S(1)}) custom-call(bf16[384,2048]{1,0:T(8,128)(2,1)} %w_gate.1, bf16[16,384]{1,0:T(8,128)(2,1)} %bitcast.4, bf16[16,2048]{1,0:T(8,128)(2,1)} %high_gate.1, bf16[384,2048]{1,0:T(8,128)(2,1)} %w_up.1, bf16[16,384]{1,0:T(8,128)(2,1)} %bitcast.5, ...), custom_call_target="tpu_custom_call" | custom-call | tf_op jit(solution)/shard_map/pallas_call | solution.py:205
  111.2 8.5 %shard_map.104 = (bf16[2048,3072]{1,0:T(8,128)(2,1)}, bf16[2048,3072]{1,0:T(8,128)(2,1)}) custom-call(bf16[8,2,2048,384]{3,2,1,0:T(8,128)(2,1)S(1)} %get-tuple-element.7.held), custom_call_target="tpu_custom_call" | custom-call | tf_op jit(solution)/shard_map/pallas_call | solution.py:231
  119.8 0.1 convert_reduce_fusion
  119.8 0.7 convert_element_type.7
